TPU v7x, 32 devices: a whole 2x2x4 slice. The times are simulated.
32 devices in a mesh: dp: 1, tp: 32 (over x, y, z, core).
Axes of the slice: x: 2, y: 2, z: 4, core: 2. Of those that a mesh axis runs over, the one named last changes fastest.
Arguments:
- x: bfloat16 [2048, 8192], P('dp')
- w_gate: bfloat16 [8192, 28672], P(None, 'tp')
- w_up: bfloat16 [8192, 28672], P(None, 'tp')
- w_down: bfloat16 [28672, 8192], P('tp')
Outputs:
- output: bfloat16 [2048, 8192], P('dp')
All inputs are finite; a program needn't handle non-finite values.
Results may differ from a plain program's by a relative error of at most 0.016.
Values are sent between devices in bfloat16 or wider.
A program may use at most 2 GiB of HBM per device.

v0:
```python
import jax
import jax.numpy as jnp
from jax import lax
from jax.sharding import PartitionSpec as P


def solution(mesh):
    def step(x, w_gate, w_up, w_down):
        gate = jnp.dot(x, w_gate, preferred_element_type=jnp.float32)
        up = jnp.dot(x, w_up, preferred_element_type=jnp.float32)
        hidden = (jax.nn.silu(gate) * up).astype(jnp.bfloat16)
        term = jnp.dot(hidden, w_down, preferred_element_type=jnp.float32).astype(jnp.bfloat16)
        return lax.psum(term, "tp")

    return jax.shard_map(
        step,
        mesh=mesh,
        in_specs=(P("dp", None), P(None, "tp"), P(None, "tp"), P("tp", None)),
        out_specs=P("dp", None),
        check_vma=False,
    )
```

profile of v0, /device:TPU:0, one launch (start us, length us, event | category | flops | bytes accessed | tf_op | source)
XLA Modules:
  0.0 663.6 jit_solution(16067537733484069344)
XLA Ops:
  6.5 0.0 all-reduce.2.cloned.1.call-start
  6.5 41.1 %fusion = f32[2048,896]{1,0:T(8,128)S(1)} fusion(bf16[2048,8192]{1,0:T(8,128)(2,1)} %param.4, bf16[8192,896]{1,0:T(8,128)(2,1)} %param.5), kind=kOutput, calls=%fused_computation.2 | convolution fusion | flops 30064771072 | bytes 55574528 | tf_op jit(solution)/shard_map/dot_general | solution.py:9
  47.6 43.3 %multiply_convert_fusion = bf16[2048,896]{1,0:T(8,128)(2,1)S(1)} fusion(f32[2048,896]{1,0:T(8,128)S(1)} %fusion, bf16[2048,8192]{1,0:T(8,128)(2,1)} %param.4, bf16[8192,896]{1,0:T(8,128)(2,1)} %param.6), kind=kOutput, calls=%fused_computation.1 | convolution fusion | flops 30075781120 | bytes 59244544 | tf_op jit(solution)/shard_map/dot_general | solution.py:10
  90.9 44.6 %convolution_convert_fusion = bf16[2048,8192]{1,0:T(8,128)(2,1)} fusion(bf16[2048,896]{1,0:T(8,128)(2,1)S(1)} %multiply_convert_fusion, bf16[896,8192]{1,0:T(8,128)(2,1)} %param.7), kind=kOutput, calls=%fused_computation | convolution fusion | flops 30081548288 | bytes 51904512 | tf_op jit(solution)/shard_map/dot_general | solution.py:12
  135.5 0.0 all-reduce.2.cloned.1.call-update
  135.5 498.3 %all-reduce.2.cloned.1.call-done = bf16[2048,8192]{1,0:T(8,128)(2,1)} async-done(((bf16[2048,8192]{1,0:T(8,128)(2,1)}), bf16[2048,8192]{1,0:T(8,128)(2,1)}) %all-reduce.2.cloned.1.call-update) | async-done | bytes 33554448 | tf_op jit(solution)/shard_map/psum | solution.py:13
  633.8 23.0 %copy.6 = bf16[2048,8192]{1,0:T(8,128)(2,1)} copy(bf16[2048,8192]{1,0:T(8,128)(2,1)} %all-reduce.2.cloned.1.call-done) | data formatting | bytes 67108864
Async XLA Ops:
  6.5 627.2 %all-reduce.2.cloned.1.call-start = ((), (), s32[]{:S(2)}) async-start(), calls=%async_computation | async-start | bytes 67108864 | tf_op jit(solution)/shard_map/psum | solution.py:13
Sparse Core Ops, SparseCore 0:
  135.6 498.0 all-reduce.1
where the time goes:
time: 664 us
  waiting for transfers between devices  498 us (75%)
  matrix products  129 us (19%)
  local copies, waits for them, and re-layouts  23 us (3%)
  between operations  13.4 us (2%)
    psum x1, waiting for transfers between devices, step(): return lax.psum(term, 'tp')  498 us
    dot_general x1, matrix products, step(): jnp.dot(hidden, w_down, preferred_element_type=jnp.float32)  44.6 us
    dot_general x1, matrix products, step(): up = jnp.dot(x, w_up, preferred_element_type=jnp.float32)  43.3 us
    dot_general x1, matrix products, step(): gate = jnp.dot(x, w_gate, preferred_element_type=jnp.float32)  41.1 us
    unnamed x1, local copies, waits for them, and re-layouts  23 us
  transfers between devices with their start and end apart: 1, of which 1 were waited for; matrix products, arithmetic and copies ran while one was open for 0% of the time, Pallas kernels for 0%

commit v1 on v0

v1 whole, which is shorter than its diff:
```python
import functools

import jax
import jax.numpy as jnp
from jax import lax
from jax.experimental import pallas as pl
from jax.experimental.pallas import tpu as pltpu
from jax.sharding import PartitionSpec as P

MESH = pl.DeviceIdType.MESH
F32, BF16 = jnp.float32, jnp.bfloat16
ROWS, D, F = 2048, 8192, 896
RB, KB, CB = 512, 1024, 1024
NK, NC = D // KB, D // CB
TILES = (ROWS // RB) * NC
SLOTS = 16
ZSLOTS = 8
LAG = (1, 3, 5, 7, 9, 11, 13, 15, 17, 19, 21, 22)
STEPS = NK + TILES + 2 + (max(LAG) + 1) // 2


def kernel(
    x, wg, wu, wd, out,
    x_buf, gu_buf, wd_buf, acc, hid,
    own, d_send, d_recv, f_send, f_keep, f_recv, zacc, z_send, z_recv, l_send, l_recv, y_buf,
    load_sem, ds_sem, dr_sem, fs_sem, fr_sem, zs_sem, zr_sem, ls_sem, lr_sem, yl_sem,
    als_sem, alr_sem, azs_sem, azr_sem, afs_sem, afr_sem, ads_sem, adr_sem,
):
    me = lax.axis_index("tp")
    core = lax.rem(me, 2)
    z = lax.rem(lax.div(me, 2), 4)
    yy = lax.rem(lax.div(me, 8), 2)
    xx = lax.div(me, 16)
    peer_core = me + 1 - 2 * core
    peer_x = me + 16 - 32 * xx
    peer_y = me + 8 - 16 * yy
    toward = (me + 2, me - 2)
    first, last = (xx, yy), (yy, xx)
    first_peer, last_peer = (peer_x, peer_y), (peer_y, peer_x)

    barrier = pltpu.get_barrier_semaphore()

    def greet(device):
        pl.semaphore_signal(barrier, inc=1, device_id={"tp": device}, device_id_type=MESH)

    greet(peer_core)
    greet(peer_x)
    greet(peer_y)

    @pl.when(z < 3)
    def _():
        greet(me + 2)

    @pl.when(z > 0)
    def _():
        greet(me - 2)

    pl.semaphore_wait(barrier, 3 + jnp.where(z < 3, 1, 0) + jnp.where(z > 0, 1, 0))

    def remote(src, dst, send_sem, recv_sem, device):
        return pltpu.make_async_remote_copy(
            src_ref=src, dst_ref=dst, send_sem=send_sem, recv_sem=recv_sem,
            device_id={"tp": device}, device_id_type=MESH,
        )

    def block(c, row, rows):
        start = pl.multiple_of(lax.div(c, NC) * RB + row, 8)
        return out.at[pl.ds(start, rows), pl.ds(pl.multiple_of(lax.rem(c, NC) * CB, CB), CB)]

    def d_copy(c):
        return remote(d_send.at[c % 2], d_recv.at[c % SLOTS], ds_sem.at[c % 2], dr_sem.at[c % SLOTS], peer_core)

    def f_copy(c, k):
        return remote(
            f_send.at[c % 2, k], f_recv.at[c % SLOTS, k], fs_sem.at[k, c % 2], fr_sem.at[k, c % SLOTS], first_peer[k]
        )

    def z_copy(c, way, s):
        return remote(
            z_send.at[way, s - 1, c % 2], z_recv.at[way, s - 1, c % SLOTS],
            zs_sem.at[way * 3 + s - 1, c % 2], zr_sem.at[way * 3 + s - 1, c % SLOTS], toward[way],
        )

    def l_copy(c, k):
        return remote(
            l_send.at[c % 2, k], l_recv.at[c % SLOTS, k], ls_sem.at[k, c % 2], lr_sem.at[k, c % SLOTS], last_peer[k]
        )

    def y_local(c, k):
        rows = block(c, core * 256 + k * 128 + first[k] * 64 + z * 16 + last[k] * 8, 8)
        return pltpu.make_async_copy(y_buf.at[c % 2, k], rows, yl_sem.at[k, c % 2])

    def al_copy(c, k, half):
        rows = block(c, core * 256 + k * 128 + first[k] * 64 + z * 16 + half * 8, 8)
        return remote(y_buf.at[c % 2, k], rows, als_sem.at[k, c % 2], alr_sem.at[k, c % SLOTS], last_peer[k])

    def az_copy(c, way, s, k, piece):
        rows = block(c, core * 256 + k * 128 + first[k] * 64 + piece * 16, 16)
        i = (way * 3 + s - 1) * 2 + k
        return remote(rows, rows, azs_sem.at[i, c % 2], azr_sem.at[i, c % SLOTS], toward[way])

    def af_copy(c, k, half):
        rows = block(c, core * 256 + k * 128 + half * 64, 64)
        return remote(rows, rows, afs_sem.at[k, c % 2], afr_sem.at[k, c % SLOTS], first_peer[k])

    def ad_copy(c, half):
        rows = block(c, half * 256, 256)
        return remote(rows, rows, ads_sem.at[c % 2], adr_sem.at[c % SLOTS], peer_core)

    def z_piece(way, s):
        piece = 4 - s + z if way == 0 else z + s - 4
        ok = (z <= 2) & (piece <= 3) if way == 0 else (z >= 1) & (piece >= 0)
        return piece, ok

    def z_got(way, s):
        piece = 3 - s + z if way == 0 else z + s - 3
        ok = (z >= 1) & (piece <= 3) if way == 0 else (z <= 2) & (piece >= 0)
        return piece, ok

    def z_go(c, s):
        for way in range(2):
            piece, ok = z_piece(way, s)

            @pl.when(ok)
            def _():
                z_send[way, s - 1, c % 2] = zacc[c % ZSLOTS, piece].astype(BF16)
                z_copy(c, way, s).start()

    def z_free(c, s):
        for way in range(2):
            piece, ok = z_piece(way, s)

            @pl.when(ok)
            def _():
                z_copy(c, way, s).wait_send()

    def r0(c):
        d_copy(c).wait_recv()
        for k in range(2):
            rows = pl.ds(pl.multiple_of(k * 128 + (1 - first[k]) * 64, 64), 64)
            f_send[c % 2, k] = (own[c % 2, rows] + d_recv[c % SLOTS, rows].astype(F32)).astype(BF16)
            f_copy(c, k).start()
        for k in range(2):
            rows = pl.ds(pl.multiple_of(k * 128 + first[k] * 64, 64), 64)
            f_keep[c % 2, k] = own[c % 2, rows] + d_recv[c % SLOTS, rows].astype(F32)

    def r0_free(c):
        for k in range(2):
            f_copy(c, k).wait_send()

    def r1(c):
        for k in range(2):
            f_copy(c, k).wait_recv()
            for j in range(4):
                rows = pl.ds(j * 16, 16)
                zacc[c % ZSLOTS, j, k] = f_keep[c % 2, k, rows] + f_recv[c % SLOTS, k, rows].astype(F32)
        z_go(c, 1)

    def rz(s):
        def stage(c):
            for way in range(2):
                piece, ok = z_got(way, s)

                @pl.when(ok)
                def _():
                    z_copy(c, way, s).wait_recv()
                    zacc[c % ZSLOTS, piece] = (
                        zacc[c % ZSLOTS, piece] + z_recv[way, s - 1, c % SLOTS].astype(F32)
                    )

            if s < 3:
                z_go(c, s + 1)
                return
            for k in range(2):
                rows = pl.ds(pl.multiple_of((1 - last[k]) * 8, 8), 8)
                l_send[c % 2, k] = zacc[c % ZSLOTS, z, k, rows].astype(BF16)
                l_copy(c, k).start()

        return stage

    def l_free(c):
        for k in range(2):
            l_copy(c, k).wait_send()

    def r5(c):
        for k in range(2):
            l_copy(c, k).wait_recv()
            rows = pl.ds(pl.multiple_of(last[k] * 8, 8), 8)
            y_buf[c % 2, k] = (zacc[c % ZSLOTS, z, k, rows] + l_recv[c % SLOTS, k].astype(F32)).astype(BF16)
            y_local(c, k).start()
            al_copy(c, k, last[k]).start()

    def r5_free(c):
        for k in range(2):
            al_copy(c, k, last[k]).wait_send()

    def az_piece(way, s):
        piece = z - (s - 1) if way == 0 else z + (s - 1)
        ok = (z <= 2) & (piece >= 0) if way == 0 else (z >= 1) & (piece <= 3)
        return piece, ok

    def az_go(c, s):
        for way in range(2):
            piece, ok = az_piece(way, s)

            @pl.when(ok)
            def _():
                for k in range(2):
                    az_copy(c, way, s, k, piece).start()

    def az_free(c, s):
        for way in range(2):
            piece, ok = az_piece(way, s)

            @pl.when(ok)
            def _():
                for k in range(2):
                    az_copy(c, way, s, k, piece).wait_send()

    def a0(c):
        for k in range(2):
            y_local(c, k).wait()
            al_copy(c, k, 1 - last[k]).wait_recv()
        az_go(c, 1)

    def az(s):
        def stage(c):
            for way in range(2):
                piece = z - s if way == 0 else z + s
                ok = piece >= 0 if way == 0 else piece <= 3

                @pl.when(ok)
                def _():
                    for k in range(2):
                        az_copy(c, way, s, k, piece).wait_recv()

            if s < 3:
                az_go(c, s + 1)
                return
            for k in range(2):
                af_copy(c, k, first[k]).start()

        return stage

    def af_free(c):
        for k in range(2):
            af_copy(c, k, first[k]).wait_send()

    def a4(c):
        for k in range(2):
            af_copy(c, k, 1 - first[k]).wait_recv()
        ad_copy(c, core).start()

    def a4_free(c):
        ad_copy(c, core).wait_send()

    def a5(c):
        ad_copy(c, 1 - core).wait_recv()

    stages = (
        (r0, r0_free),
        (r1, lambda c: z_free(c, 1)),
        (rz(1), lambda c: z_free(c, 2)),
        (rz(2), lambda c: z_free(c, 3)),
        (rz(3), l_free),
        (r5, r5_free),
        (a0, lambda c: az_free(c, 1)),
        (az(1), lambda c: az_free(c, 2)),
        (az(2), lambda c: az_free(c, 3)),
        (az(3), af_free),
        (a4, a4_free),
        (a5, None),
    )

    def comm(t, part):
        for lag, (stage, free) in zip(LAG, stages):
            if lag % 2 != part:
                continue
            c = t - NK - lag // 2
            if free is not None:

                @pl.when((c >= 2) & (c < TILES + 2))
                def _():
                    free(c - 2)

            @pl.when((c >= 0) & (c < TILES))
            def _():
                stage(c)

    def loads(t):
        p = t % 2
        rows = pl.ds(pl.multiple_of(lax.div(t, NK) * RB, RB), RB)
        deep = pl.ds(pl.multiple_of(lax.rem(t, NK) * KB, KB), KB)
        cols = pl.ds(pl.multiple_of(lax.rem(t, NC) * CB, CB), CB)
        up = (
            pltpu.make_async_copy(x.at[rows, deep], x_buf.at[p], load_sem.at[p, 0]),
            pltpu.make_async_copy(wg.at[deep], gu_buf.at[p, :, pl.ds(0, F)], load_sem.at[p, 1]),
            pltpu.make_async_copy(wu.at[deep], gu_buf.at[p, :, pl.ds(F, F)], load_sem.at[p, 2]),
        )
        down = pltpu.make_async_copy(wd.at[:, cols], wd_buf.at[p], load_sem.at[p, 3])
        return up, down

    def fetch(t):
        up, down = loads(t)

        @pl.when(t < TILES)
        def _():
            for copy in up:
                copy.start()

        @pl.when((t >= NK) & (t < NK + TILES))
        def _():
            down.start()

    acc[...] = jnp.zeros_like(acc)
    fetch(jnp.int32(0))

    def step(t, _):
        fetch(t + 1)
        up, down = loads(t)
        p = t % 2
        c = t - NK

        @pl.when((c >= 2) & (c < TILES + 2))
        def _():
            d_copy(c - 2).wait_send()

        @pl.when((c >= 0) & (c < TILES))
        def _():
            down.wait()
            w = wd_buf[p]
            d_send[c % 2] = jnp.dot(hid[1 - core], w, preferred_element_type=F32).astype(BF16)
            d_copy(c).start()
            own[c % 2] = jnp.dot(hid[core], w, preferred_element_type=F32)

        comm(t, 0)

        @pl.when(t < TILES)
        def _():
            for copy in up:
                copy.wait()
            acc[...] += jnp.dot(x_buf[p], gu_buf[p], preferred_element_type=F32)

            @pl.when(t % NK == NK - 1)
            def _():
                for half in range(2):
                    rows = pl.ds(half * 256, 256)
                    gate = acc[rows, pl.ds(0, F)]
                    hid[half] = (gate * jax.nn.sigmoid(gate) * acc[rows, pl.ds(F, F)]).astype(BF16)
                acc[...] = jnp.zeros_like(acc)

        comm(t, 1)
        return 0

    lax.fori_loop(0, STEPS, step, 0)


def block_of(x, wg, wu, wd):
    any_space = pl.BlockSpec(memory_space=pl.ANY)
    dma = pltpu.SemaphoreType.DMA
    return pl.pallas_call(
        kernel,
        out_shape=jax.ShapeDtypeStruct((ROWS, D), BF16),
        in_specs=[any_space] * 4,
        out_specs=any_space,
        scratch_shapes=[
            pltpu.VMEM((2, RB, KB), BF16),
            pltpu.VMEM((2, KB, 2 * F), BF16),
            pltpu.VMEM((2, F, CB), BF16),
            pltpu.VMEM((RB, 2 * F), F32),
            pltpu.VMEM((2, RB // 2, F), BF16),
            pltpu.VMEM((2, 256, CB), F32),
            pltpu.VMEM((2, 256, CB), BF16),
            pltpu.VMEM((SLOTS, 256, CB), BF16),
            pltpu.VMEM((2, 2, 64, CB), BF16),
            pltpu.VMEM((2, 2, 64, CB), F32),
            pltpu.VMEM((SLOTS, 2, 64, CB), BF16),
            pltpu.VMEM((ZSLOTS, 4, 2, 16, CB), F32),
            pltpu.VMEM((2, 3, 2, 2, 16, CB), BF16),
            pltpu.VMEM((2, 3, SLOTS, 2, 16, CB), BF16),
            pltpu.VMEM((2, 2, 8, CB), BF16),
            pltpu.VMEM((SLOTS, 2, 8, CB), BF16),
            pltpu.VMEM((2, 2, 8, CB), BF16),
            dma((2, 4)),
            dma((2,)), dma((SLOTS,)),
            dma((2, 2)), dma((2, SLOTS)),
            dma((6, 2)), dma((6, SLOTS)),
            dma((2, 2)), dma((2, SLOTS)),
            dma((2, 2)),
            dma((2, 2)), dma((2, SLOTS)),
            dma((12, 2)), dma((12, SLOTS)),
            dma((2, 2)), dma((2, SLOTS)),
            dma((2,)), dma((SLOTS,)),
        ],
        compiler_params=pltpu.CompilerParams(
            collective_id=0, has_side_effects=True, vmem_limit_bytes=66_000_000
        ),
    )(x, wg, wu, wd)


def solution(mesh):
    return jax.shard_map(
        block_of,
        mesh=mesh,
        in_specs=(P("dp", None), P(None, "tp"), P(None, "tp"), P("tp", None)),
        out_specs=P("dp", None),
        check_vma=False,
    )
```

time: 664 us -> 287 us (0.43)
  waiting for transfers between devices: 498 us -> 0 us
  Pallas kernels: 0 us -> 264 us
  matrix products: 129 us -> 0 us
  between operations: 13.4 us -> 0.01 us
    psum x1 -> x0, waiting for transfers between devices: 498 us -> none  [step(): return lax.psum(term, 'tp')]
    pallas_call x0 -> x1, Pallas kernels: none -> 264 us  [block_of(): pl.pallas_call(kernel, out_shape=jax.ShapeDtypeStruct((ROWS, D), BF16), i...]
    dot_general x3 -> x0, matrix products: 129 us -> none  [the longest x1 44.6 us: step(): jnp.dot(hidden, w_down, preferred_element_type=jnp.float32)]
  transfers between devices with their start and end apart: 1 -> 0, of which waited for: 1 -> 0; matrix products, arithmetic and copies ran while one was open for 0% -> 0% of each run, Pallas kernels for 0% -> 0%
where the time goes in v1:
time: 287 us
  Pallas kernels  264 us (92%)
  local copies, waits for them, and re-layouts  23 us (8%)
    pallas_call x1, Pallas kernels, block_of(): pl.pallas_call(kernel, out_shape=jax.ShapeDtypeStruct((ROWS, D), BF16), i...  264 us
    unnamed x1, local copies, waits for them, and re-layouts  23 us

profile of v1, /device:TPU:0, one launch (start us, length us, event | category | flops | bytes accessed | tf_op | source)
XLA Modules:
  0.0 286.7 jit_solution(14699622083179238827)
XLA Ops:
  0.0 263.7 %shard_map.46 = bf16[2048,8192]{1,0:T(8,128)(2,1)} custom-call(bf16[2048,8192]{1,0:T(8,128)(2,1)} %x.1, bf16[8192,896]{1,0:T(8,128)(2,1)} %wg.1, bf16[8192,896]{1,0:T(8,128)(2,1)} %wu.1, bf16[896,8192]{1,0:T(8,128)(2,1)} %wd.1), custom_call_target="tpu_custom_call" | custom-call | tf_op jit(solution)/shard_map/pallas_call | solution.py:361
  263.7 23.0 %copy.6 = bf16[2048,8192]{1,0:T(8,128)(2,1)} copy(bf16[2048,8192]{1,0:T(8,128)(2,1)} %shard_map.46) | data formatting | bytes 67108864

commit v2 on v1

v2 whole, which is shorter than its diff:
```python
import jax
import jax.numpy as jnp
from jax import lax
from jax.experimental import pallas as pl
from jax.experimental.pallas import tpu as pltpu
from jax.sharding import PartitionSpec as P

MESH = pl.DeviceIdType.MESH
F32, BF16 = jnp.float32, jnp.bfloat16
ROWS, D, F = 2048, 8192, 896
RB, KB, CB = 256, 1024, 1024
NK, NC = D // KB, D // CB
TILES = (ROWS // RB) * NC
SLOTS = 24
SENDS = 4
ZSLOTS = 6
HBM_ROWS = 512
JOIN = 4
HBM_TILES = HBM_ROWS // RB * NC
HALF, QUARTER, EIGHTH, PIECE = RB // 2, RB // 4, RB // 8, RB // 32
LAG = (2, 6, 9, 11, 14, 18, 21, 24, 26, 34, 36)
STEPS = NK + TILES + SENDS + max(LAG) // 2 + 1


def kernel(
    x, wg, wu, wd, out_h, out_v,
    x_buf, gu_buf, wd_buf, acc, hid, term,
    own, d_send, d_recv, f_send, f_keep, f_recv, zacc, z_send, z_recv, l_send, l_recv, y_buf,
    load_sem, ds_sem, dr_sem, fs_sem, fr_sem, zs_sem, zr_sem, ls_sem, lr_sem, yl_sem,
    azs_sem, azr_sem, afs_sem, afr_sem, ads_sem, adr_sem,
):
    me = lax.axis_index("tp")
    core = lax.rem(me, 2)
    z = lax.rem(lax.div(me, 2), 4)
    yy = lax.rem(lax.div(me, 8), 2)
    xx = lax.div(me, 16)
    peer_core = me + 1 - 2 * core
    peer_x = me + 16 - 32 * xx
    peer_y = me + 8 - 16 * yy
    toward = (me + 2, me - 2)
    first = (xx, yy)
    first_peer, last_peer = (peer_x, peer_y), (peer_y, peer_x)

    barrier = pltpu.get_barrier_semaphore()

    def greet(device):
        pl.semaphore_signal(barrier, inc=1, device_id={"tp": device}, device_id_type=MESH)

    greet(peer_core)
    greet(peer_x)
    greet(peer_y)

    @pl.when(z < 3)
    def _():
        greet(me + 2)

    @pl.when(z > 0)
    def _():
        greet(me - 2)

    pl.semaphore_wait(barrier, 3 + jnp.where(z < 3, 1, 0) + jnp.where(z > 0, 1, 0))

    def remote(src, dst, send_sem, recv_sem, device):
        return pltpu.make_async_remote_copy(
            src_ref=src, dst_ref=dst, send_sem=send_sem, recv_sem=recv_sem,
            device_id={"tp": device}, device_id_type=MESH,
        )

    def block(c, row, rows, place):
        ref, base = ((out_h, 0), (out_v, HBM_ROWS))[place]
        start = pl.multiple_of(lax.div(c, NC) * RB - base + row, PIECE)
        return ref.at[pl.ds(start, rows), pl.ds(pl.multiple_of(lax.rem(c, NC) * CB, CB), CB)]

    def d_copy(c):
        return remote(d_send.at[c % SENDS], d_recv.at[c % SLOTS], ds_sem.at[c % SENDS], dr_sem.at[c % SLOTS], peer_core)

    def f_copy(c, k):
        return remote(
            f_send.at[c % SENDS, k], f_recv.at[c % SLOTS, k], fs_sem.at[k, c % SENDS], fr_sem.at[k, c % SLOTS], first_peer[k]
        )

    def z_copy(c, way, s):
        return remote(
            z_send.at[way, s - 1, c % SENDS], z_recv.at[way, s - 1, c % SLOTS],
            zs_sem.at[way * 3 + s - 1, c % SENDS], zr_sem.at[way * 3 + s - 1, c % SLOTS], toward[way],
        )

    def l_copy(c, k):
        return remote(
            l_send.at[c % SENDS, k], l_recv.at[c % SLOTS, k], ls_sem.at[k, c % SENDS], lr_sem.at[k, c % SLOTS], last_peer[k]
        )

    def piece_of(c, k, piece, place):
        return block(c, core * HALF + k * QUARTER + first[k] * EIGHTH + piece * PIECE, PIECE, place)

    def y_local(c, k):
        return pltpu.make_async_copy(y_buf.at[c % SENDS, k], piece_of(c, k, z, 0), yl_sem.at[k, c % SENDS])

    def az_copy(c, way, s, k, piece, place):
        rows = piece_of(c, k, piece, place)
        i = (way * 3 + s - 1) * 2 + k
        src = y_buf.at[c % SENDS, k] if s == 1 else rows
        return remote(src, rows, azs_sem.at[i, c % SENDS], azr_sem.at[i, c % SLOTS], toward[way])

    def af_copy(c, k, half, place):
        rows = block(c, core * HALF + k * QUARTER + half * EIGHTH, EIGHTH, place)
        return remote(rows, rows, afs_sem.at[k, c % SENDS], afr_sem.at[k, c % SLOTS], first_peer[k])

    def ad_copy(c, half, place):
        rows = block(c, half * HALF, HALF, place)
        return remote(rows, rows, ads_sem.at[c % SENDS], adr_sem.at[c % SLOTS], peer_core)

    def z_piece(way, s):
        piece = 4 - s + z if way == 0 else z + s - 4
        ok = (z <= 2) & (piece <= 3) if way == 0 else (z >= 1) & (piece >= 0)
        return piece, ok

    def z_got(way, s):
        piece = 3 - s + z if way == 0 else z + s - 3
        ok = (z >= 1) & (piece <= 3) if way == 0 else (z <= 2) & (piece >= 0)
        return piece, ok

    def z_go(c, s):
        for way in range(2):
            piece, ok = z_piece(way, s)

            @pl.when(ok)
            def _():
                z_send[way, s - 1, c % SENDS] = zacc[c % ZSLOTS, piece].astype(BF16)
                z_copy(c, way, s).start()

    def z_free(s):
        def free(c, place):
            for way in range(2):
                piece, ok = z_piece(way, s)

                @pl.when(ok)
                def _():
                    z_copy(c, way, s).wait_send()

        return free

    def r0(c, place):
        d_copy(c).wait_recv()
        for k in range(2):
            rows = pl.ds(pl.multiple_of(k * QUARTER + (1 - first[k]) * EIGHTH, EIGHTH), EIGHTH)
            f_send[c % SENDS, k] = (own[c % 3, rows] + d_recv[c % SLOTS, rows].astype(F32)).astype(BF16)
            f_copy(c, k).start()
        for k in range(2):
            rows = pl.ds(pl.multiple_of(k * QUARTER + first[k] * EIGHTH, EIGHTH), EIGHTH)
            f_keep[c % SENDS, k] = own[c % 3, rows] + d_recv[c % SLOTS, rows].astype(F32)

    def r0_free(c, place):
        for k in range(2):
            f_copy(c, k).wait_send()

    def r1(c, place):
        for k in range(2):
            f_copy(c, k).wait_recv()
            for j in range(4):
                rows = pl.ds(j * PIECE, PIECE)
                zacc[c % ZSLOTS, j, k] = f_keep[c % SENDS, k, rows] + f_recv[c % SLOTS, k, rows].astype(F32)
        z_go(c, 1)

    def rz(s):
        def stage(c, place):
            for way in range(2):
                piece, ok = z_got(way, s)

                @pl.when(ok)
                def _():
                    z_copy(c, way, s).wait_recv()
                    zacc[c % ZSLOTS, piece] = (
                        zacc[c % ZSLOTS, piece] + z_recv[way, s - 1, c % SLOTS].astype(F32)
                    )

            if s < 3:
                z_go(c, s + 1)
                return
            for k in range(2):
                l_send[c % SENDS, k] = zacc[c % ZSLOTS, z, k].astype(BF16)
                l_copy(c, k).start()

        return stage

    def az_piece(way, s):
        piece = z - (s - 1) if way == 0 else z + (s - 1)
        ok = (z <= 2) & (piece >= 0) if way == 0 else (z >= 1) & (piece <= 3)
        return piece, ok

    def az_go(c, s, place):
        for way in range(2):
            piece, ok = az_piece(way, s)

            @pl.when(ok)
            def _():
                for k in range(2):
                    az_copy(c, way, s, k, piece, place).start()

    def az_free(s):
        def free(c, place):
            for way in range(2):
                piece, ok = az_piece(way, s)

                @pl.when(ok)
                def _():
                    for k in range(2):
                        az_copy(c, way, s, k, piece, place).wait_send()

        return free

    def l_go(c, place):
        for k in range(2):
            l_copy(c, k).wait_recv()
            y = (l_send[c % SENDS, k].astype(F32) + l_recv[c % SLOTS, k].astype(F32)).astype(BF16)
            y_buf[c % SENDS, k] = y
            if place == 0:
                y_local(c, k).start()
            else:
                piece_of(c, k, z, place)[...] = y
        az_go(c, 1, place)

    def l_free(c, place):
        for k in range(2):
            l_copy(c, k).wait_send()

    def az(s):
        def stage(c, place):
            for way in range(2):
                piece = z - s if way == 0 else z + s
                ok = piece >= 0 if way == 0 else piece <= 3

                @pl.when(ok)
                def _():
                    for k in range(2):
                        az_copy(c, way, s, k, piece, place).wait_recv()

            if s == 1 and place == 0:
                for k in range(2):
                    y_local(c, k).wait()
            if s < 3:
                az_go(c, s + 1, place)
                return
            for k in range(2):
                af_copy(c, k, first[k], place).start()

        return stage

    def af_free(c, place):
        for k in range(2):
            af_copy(c, k, first[k], place).wait_send()

    def a4(c, place):
        for k in range(2):
            af_copy(c, k, 1 - first[k], place).wait_recv()
        ad_copy(c, core, place).start()

    def a4_free(c, place):
        ad_copy(c, core, place).wait_send()

    def a5(c, place):
        ad_copy(c, 1 - core, place).wait_recv()

    stages = (
        (r0, r0_free, False),
        (r1, z_free(1), False),
        (rz(1), z_free(2), False),
        (rz(2), z_free(3), False),
        (rz(3), l_free, False),
        (l_go, az_free(1), True),
        (az(1), az_free(2), True),
        (az(2), az_free(3), True),
        (az(3), af_free, True),
        (a4, a4_free, True),
        (a5, None, True),
    )

    def at_place(c, ok, split, f):
        if not split:

            @pl.when(ok)
            def _():
                f(c, 0)

            return
        for place in range(2):

            @pl.when(ok & ((c < HBM_TILES) if place == 0 else (c >= HBM_TILES)))
            def _():
                f(c, place)

    def comm(u, part):
        for lag, (stage, free, split) in zip(LAG, stages):
            if lag % 2 != part:
                continue
            c = u - NK - lag // 2
            if free is not None:
                at_place(c - SENDS, (c >= SENDS) & (c < TILES + SENDS), split, free)
            at_place(c, (c >= 0) & (c < TILES), split, stage)

    def loads(u):
        p = u % 2
        rows = pl.ds(pl.multiple_of(lax.div(u, NK) * RB, RB), RB)
        deep = pl.ds(pl.multiple_of(lax.rem(u, NK) * KB, KB), KB)
        cols = pl.ds(pl.multiple_of(lax.rem(u, NC) * CB, CB), CB)
        up = (
            pltpu.make_async_copy(x.at[rows, deep], x_buf.at[p], load_sem.at[p, 0]),
            pltpu.make_async_copy(wg.at[deep], gu_buf.at[p, :, pl.ds(0, F)], load_sem.at[p, 1]),
            pltpu.make_async_copy(wu.at[deep], gu_buf.at[p, :, pl.ds(F, F)], load_sem.at[p, 2]),
        )
        down = pltpu.make_async_copy(wd.at[:, cols], wd_buf.at[p], load_sem.at[p, 3])
        return up, down

    def fetch(u):
        up, down = loads(u)

        @pl.when(u < TILES)
        def _():
            for copy in up:
                copy.start()

        @pl.when((u >= NK) & (u < NK + TILES))
        def _():
            down.start()

    acc[...] = jnp.zeros_like(acc)
    fetch(jnp.int32(0))

    def step(u, _):
        fetch(u + 1)
        up, down = loads(u)
        p = u % 2
        c = u - NK

        @pl.when((c >= SENDS) & (c < TILES + SENDS))
        def _():
            d_copy(c - SENDS).wait_send()

        @pl.when((c >= 0) & (c < TILES))
        def _():
            down.wait()
            term[...] = jnp.dot(hid[...], wd_buf[p], preferred_element_type=F32)
            d_send[c % SENDS] = term[pl.ds(pl.multiple_of((1 - core) * HALF, HALF), HALF)].astype(BF16)
            d_copy(c).start()
            own[c % 3] = term[pl.ds(pl.multiple_of(core * HALF, HALF), HALF)]

        comm(u, 0)

        @pl.when(u < TILES)
        def _():
            for copy in up:
                copy.wait()
            acc[...] += jnp.dot(x_buf[p], gu_buf[p], preferred_element_type=F32)

            @pl.when(lax.rem(u, NK) == NK - 1)
            def _():
                gate = acc[:, pl.ds(0, F)]
                hid[...] = (gate * jax.nn.sigmoid(gate) * acc[:, pl.ds(F, F)]).astype(BF16)
                acc[...] = jnp.zeros_like(acc)

        comm(u, 1)
        return 0

    lax.fori_loop(0, STEPS, step, 0)


def join(high, low, out, buf, in_sem, out_sem, low_sem):
    rows = HBM_ROWS // JOIN
    lows = pltpu.make_async_copy(low, out.at[pl.ds(HBM_ROWS, ROWS - HBM_ROWS)], low_sem)
    ins = [pltpu.make_async_copy(high.at[pl.ds(i * rows, rows)], buf.at[i], in_sem.at[i]) for i in range(JOIN)]
    outs = [pltpu.make_async_copy(buf.at[i], out.at[pl.ds(i * rows, rows)], out_sem.at[i]) for i in range(JOIN)]
    for copy in ins:
        copy.start()
    lows.start()
    for arrived, copy in zip(ins, outs):
        arrived.wait()
        copy.start()
    for copy in outs:
        copy.wait()
    lows.wait()


def block_of(x, wg, wu, wd):
    any_space = pl.BlockSpec(memory_space=pl.ANY)
    dma = pltpu.SemaphoreType.DMA
    high, low = pl.pallas_call(
        kernel,
        out_shape=(
            jax.ShapeDtypeStruct((HBM_ROWS, D), BF16),
            pltpu.VMEM((ROWS - HBM_ROWS, D), BF16),
        ),
        in_specs=[any_space] * 4,
        out_specs=(any_space, pl.BlockSpec(memory_space=pltpu.VMEM)),
        scratch_shapes=[
            pltpu.VMEM((2, RB, KB), BF16),
            pltpu.VMEM((2, KB, 2 * F), BF16),
            pltpu.VMEM((2, F, CB), BF16),
            pltpu.VMEM((RB, 2 * F), F32),
            pltpu.VMEM((RB, F), BF16),
            pltpu.VMEM((RB, CB), F32),
            pltpu.VMEM((3, HALF, CB), F32),
            pltpu.VMEM((SENDS, HALF, CB), BF16),
            pltpu.VMEM((SLOTS, HALF, CB), BF16),
            pltpu.VMEM((SENDS, 2, EIGHTH, CB), BF16),
            pltpu.VMEM((SENDS, 2, EIGHTH, CB), F32),
            pltpu.VMEM((SLOTS, 2, EIGHTH, CB), BF16),
            pltpu.VMEM((ZSLOTS, 4, 2, PIECE, CB), F32),
            pltpu.VMEM((2, 3, SENDS, 2, PIECE, CB), BF16),
            pltpu.VMEM((2, 3, SLOTS, 2, PIECE, CB), BF16),
            pltpu.VMEM((SENDS, 2, PIECE, CB), BF16),
            pltpu.VMEM((SLOTS, 2, PIECE, CB), BF16),
            pltpu.VMEM((SENDS, 2, PIECE, CB), BF16),
            dma((2, 4)),
            dma((SENDS,)), dma((SLOTS,)),
            dma((2, SENDS)), dma((2, SLOTS)),
            dma((6, SENDS)), dma((6, SLOTS)),
            dma((2, SENDS)), dma((2, SLOTS)),
            dma((2, SENDS)),
            dma((12, SENDS)), dma((12, SLOTS)),
            dma((2, SENDS)), dma((2, SLOTS)),
            dma((SENDS,)), dma((SLOTS,)),
        ],
        compiler_params=pltpu.CompilerParams(
            collective_id=0, has_side_effects=True, vmem_limit_bytes=40_000_000
        ),
    )(x, wg, wu, wd)
    low = pltpu.with_memory_space_constraint(low, pltpu.VMEM)
    return pl.pallas_call(
        join,
        out_shape=jax.ShapeDtypeStruct((ROWS, D), BF16),
        in_specs=[any_space] * 2,
        out_specs=any_space,
        scratch_shapes=[
            pltpu.VMEM((JOIN, HBM_ROWS // JOIN, D), BF16),
            dma((JOIN,)), dma((JOIN,)), dma,
        ],
        compiler_params=pltpu.CompilerParams(vmem_limit_bytes=24_000_000),
    )(high, low)


def solution(mesh):
    return jax.shard_map(
        block_of,
        mesh=mesh,
        in_specs=(P("dp", None), P(None, "tp"), P(None, "tp"), P("tp", None)),
        out_specs=P("dp", None),
        check_vma=False,
    )
```

time: 287 us -> 272 us (0.948)
  local copies, waits for them, and re-layouts: 23 us -> 0 us
  Pallas kernels: 264 us -> 272 us
    unnamed x1 -> x0, local copies, waits for them, and re-layouts: 23 us -> none
    pallas_call x1 -> x2, Pallas kernels: 264 us -> 272 us  [the longest x1 258 us: block_of(): pl.pallas_call(kernel, out_shape=(jax.ShapeDtypeStruct((HBM_ROWS, D), BF1...]
where the time goes in v2:
time: 272 us
  Pallas kernels  272 us (100%)
    pallas_call x1, Pallas kernels, block_of(): pl.pallas_call(kernel, out_shape=(jax.ShapeDtypeStruct((HBM_ROWS, D), BF1...  258 us
    pallas_call x1, Pallas kernels, block_of(): pl.pallas_call(join, out_shape=jax.ShapeDtypeStruct((ROWS, D), BF16), in_...  13.9 us

profile of v2, /device:TPU:0, one launch (start us, length us, event | category | flops | bytes accessed | tf_op | source)
XLA Modules:
  0.0 271.9 jit_solution(3412220365046371495)
XLA Ops:
  0.0 258.0 %shard_map.46 = (bf16[512,8192]{1,0:T(8,128)(2,1)}, bf16[1536,8192]{1,0:T(8,128)(2,1)S(1)}) custom-call(bf16[2048,8192]{1,0:T(8,128)(2,1)} %x.1, bf16[8192,896]{1,0:T(8,128)(2,1)} %wg.1, bf16[8192,896]{1,0:T(8,128)(2,1)} %wu.1, bf16[896,8192]{1,0:T(8,128)(2,1)} %wd.1), custom_call_target="tpu_custom_call" | custom-call | tf_op jit(solution)/shard_map/pallas_call | solution.py:386
  258.0 13.9 %shard_map.47 = bf16[2048,8192]{1,0:T(8,128)(2,1)} custom-call(bf16[512,8192]{1,0:T(8,128)(2,1)} %get-tuple-element.7.high, bf16[1536,8192]{1,0:T(8,128)(2,1)S(1)} %get-tuple-element.8.low), custom_call_target="tpu_custom_call" | custom-call | tf_op jit(solution)/shard_map/pallas_call | solution.py:428

commit v3 on v2

--- a/solution.py
+++ b/solution.py
@@ -18,7 +18,7 @@
 JOIN = 4
 HBM_TILES = HBM_ROWS // RB * NC
 HALF, QUARTER, EIGHTH, PIECE = RB // 2, RB // 4, RB // 8, RB // 32
-LAG = (2, 6, 9, 11, 14, 18, 21, 24, 26, 34, 36)
+LAG = (2, 5, 7, 10, 13, 16, 20, 23, 26, 38, 41)
 STEPS = NK + TILES + SENDS + max(LAG) // 2 + 1
 
 
@@ -58,7 +58,7 @@
     def _():
         greet(me - 2)
 
-    pl.semaphore_wait(barrier, 3 + jnp.where(z < 3, 1, 0) + jnp.where(z > 0, 1, 0))
+    greeted = 3 + jnp.where(z < 3, 1, 0) + jnp.where(z > 0, 1, 0)
 
     def remote(src, dst, send_sem, recv_sem, device):
         return pltpu.make_async_remote_copy(
@@ -331,6 +331,10 @@
         up, down = loads(u)
         p = u % 2
         c = u - NK
+
+        @pl.when(c == 0)
+        def _():
+            pl.semaphore_wait(barrier, greeted)
 
         @pl.when((c >= SENDS) & (c < TILES + SENDS))
         def _():

time: 272 us -> 270 us (level)
  no operation moved by 1% of the time
where the time goes in v3:
time: 270 us
  Pallas kernels  270 us (100%)
    pallas_call x1, Pallas kernels, block_of(): pl.pallas_call(kernel, out_shape=(jax.ShapeDtypeStruct((HBM_ROWS, D), BF1...  256 us
    pallas_call x1, Pallas kernels, block_of(): pl.pallas_call(join, out_shape=jax.ShapeDtypeStruct((ROWS, D), BF16), in_...  13.9 us

profile of v3, /device:TPU:0, one launch (start us, length us, event | category | flops | bytes accessed | tf_op | source)
XLA Modules:
  0.0 269.9 jit_solution(12574158682854408700)
XLA Ops:
  0.0 256.0 %shard_map.46 = (bf16[512,8192]{1,0:T(8,128)(2,1)}, bf16[1536,8192]{1,0:T(8,128)(2,1)S(1)}) custom-call(bf16[2048,8192]{1,0:T(8,128)(2,1)} %x.1, bf16[8192,896]{1,0:T(8,128)(2,1)} %wg.1, bf16[8192,896]{1,0:T(8,128)(2,1)} %wu.1, bf16[896,8192]{1,0:T(8,128)(2,1)} %wd.1), custom_call_target="tpu_custom_call" | custom-call | tf_op jit(solution)/shard_map/pallas_call | solution.py:390
  256.0 13.9 %shard_map.47 = bf16[2048,8192]{1,0:T(8,128)(2,1)} custom-call(bf16[512,8192]{1,0:T(8,128)(2,1)} %get-tuple-element.7.high, bf16[1536,8192]{1,0:T(8,128)(2,1)S(1)} %get-tuple-element.8.low), custom_call_target="tpu_custom_call" | custom-call | tf_op jit(solution)/shard_map/pallas_call | solution.py:432
